TPU v7x, 1024 devices: a whole 8x8x8 slice. The times are simulated.
1024 devices in a mesh: gx: 32 (over y_hi, x), gy: 8 (over z), gz: 4 (over y_lo, core).
Axes of the slice: x: 8, y: 8 (y_hi: 4, y_lo: 2; y = y_hi * 2 + y_lo), z: 8, core: 2. Of those that a mesh axis runs over, the one named last changes fastest.
Arguments:
- displacement: float32 [32, 8, 18432], P('gx', 'gy', 'gz'), may hold values from -0.1 to 0.1
- species: int32 [32, 8, 6144], P('gx', 'gy', 'gz'), may hold values from 0 to 1
- centres: int32 [32, 8, 64], P('gx', 'gy', 'gz'), may hold values from 0 to 1535, as said below
- neighbours: int32 [32, 8, 2048], P('gx', 'gy', 'gz'), may hold values from 0 to 5183, as said below
- neighbour_count: int32 [32, 8, 64], P('gx', 'gy', 'gz'), may hold values from 1 to 32, as said below
- live_centres: int32 [32, 8, 4], P('gx', 'gy', 'gz'), may hold values from 8 to 16, as said below
- w_two: float32 [12, 64], replicated, may hold values from -1.75 to 1.75
- w_lat: float32 [64, 64], replicated, may hold values from -0.75 to 0.75
- w_env: float32 [64, 64], replicated, may hold values from -0.75 to 0.75
- w_out: float32 [256, 64], replicated, may hold values from -0.375 to 0.375
- readout: float32 [64], replicated, may hold values from -0.75 to 0.75
Outputs:
- centre_energy: float32 [32, 8, 64], P('gx', 'gy', 'gz')
- forces: float32 [32, 8, 18432], P('gx', 'gy', 'gz')
Inputs may be any that keep to these rules, and one draw needn't show every extreme that they name: `centres`: local atom index of an owned atom; entries may repeat. `neighbours`: extended index of an atom whose cell lies within two cells of the centre's cell in each dimension, with squared cell distance at most 4; never the centre itself. `neighbour_count`: in every domain some centre has all 32 slots live. `live_centres`: some domain has all 16 centres live; the live centres are the first ones.
All inputs are finite; a program needn't handle non-finite values.
Results may differ from a plain program's by a relative error of at most 0.0003.
Values sent between devices are 32-bit elements; how exact they have to be, the bound alone decides.
No kernel may reach another device: no remote copies, remote signals or barrier semaphores. Data moves between devices by JAX's collectives and lax.ppermute only.
A program may use at most 32 MiB of HBM per device.

v0:
```python
import math

import jax
import jax.numpy as jnp
import numpy as np
from jax import lax
from jax.experimental import pallas as pl
from jax.experimental.pallas import tpu as pltpu
from jax.sharding import PartitionSpec as P

F32 = jnp.float32
BF16 = jnp.bfloat16
CELL = 3.1
CUT = 6.0
VM = pl.BlockSpec(memory_space=pltpu.VMEM)
SM = pl.BlockSpec(memory_space=pltpu.SMEM)
HB = pl.BlockSpec(memory_space=pltpu.HBM)
PAIRS = 512
NS = 16
LIST = 40


def call(kernel, outs, ins, name, scratch=(), flops=0, mib=2):
    specs = [s for _, s in ins]
    return pl.pallas_call(
        kernel,
        out_shape=outs,
        in_specs=specs,
        out_specs=jax.tree.map(lambda _: VM, outs),
        scratch_shapes=list(scratch),
        name=name,
        compiler_params=pltpu.CompilerParams(vmem_limit_bytes=mib << 20),
        cost_estimate=pl.CostEstimate(flops=flops, bytes_accessed=0, transcendentals=0),
    )(*[a for a, _ in ins])


def split(v, parts):
    out = []
    for _ in range(parts - 1):
        h = v.astype(BF16)
        out.append(h)
        v = v - h.astype(F32)
    out.append(v.astype(BF16))
    return out


def mm(a, b, dims=((1,), (0,))):
    return lax.dot_general(a, b, (dims, ((), ())), preferred_element_type=F32)


def pack_kernel(d_in, s_in, nb_in, ce_in, ct_in, al_ref, o_ref, t_ref, d_ref, s_ref, nb_ref, ce_ref, ct_ref, sem):
    refs = (d_ref, s_ref, nb_ref, ce_ref, ct_ref)
    copies = [
        pltpu.make_async_copy(a, b, sem.at[i])
        for i, (a, b) in enumerate(zip((d_in, s_in, nb_in, ce_in, ct_in), refs))
    ]
    for c in copies:
        c.start()
    o_ref[48 : 48 + LIST, :] = jnp.zeros((LIST, 128), F32)
    t_ref[...] = jnp.zeros((128, 128), F32)
    for c in copies:
        c.wait()
    for i in range(36):
        o_ref[i : i + 1, :] = d_ref[0, :, 128 * i : 128 * i + 128]
    for i in range(12):
        o_ref[36 + i : 37 + i, :] = s_ref[0, :, 128 * i : 128 * i + 128].astype(F32)
    for i in range(4):
        v = nb_ref[0, :, 128 * i : 128 * i + 128].astype(F32)
        for c in range(4):
            t_ref[4 * i + c : 4 * i + c + 1, :] = pltpu.roll(v, (128 - 32 * c) % 128, axis=1)
    o_ref[48:80, 0:NS] = t_ref[...].T[0:32, 0:NS]
    lane = lax.broadcasted_iota(jnp.int32, (1, NS), 1)
    o_ref[80:81, 0:NS] = ce_ref[0].astype(F32)
    o_ref[81:82, 0:NS] = jnp.where(lane < al_ref[0], ct_ref[0], 0).astype(F32)


def zperm():
    m = np.zeros((3, 128, 256), np.float32)
    for s in range(16):
        d, z = (1, s + 4) if s < 4 else ((0, s - 4) if s < 12 else (2, s - 12))
        for a in range(3):
            at = (s // 8) * 128 + (s % 8) * 12 + a * 4
            for c in range(3):
                m[d, z * 9 + a * 3 + c, at + c] = 1.0
            m[d, 72 + z * 3 + a, at + 3] = 1.0
    return m.reshape(384, 256)


def zrows_kernel(e_ref, g_ref, p_ref, o_ref, l_ref, lo_ref, hi_ref, t_ref):
    e = e_ref[0]
    lane = lax.broadcasted_iota(jnp.int32, (4, 128), 1)
    wide = lax.broadcasted_iota(jnp.int32, (LIST, 128), 1)
    lists = jnp.zeros((LIST, 128), F32)
    for d in range(3):
        at = lax.rem(e + (0, 3, 1)[d], 4)
        for j in range(16):
            r, off = divmod(72 * j, 128)
            v = g_ref[at, pl.ds(r, 4, stride=9), :]
            v = pltpu.roll(v, (128 - off) % 128, axis=1) if off else v
            if off + 72 > 128:
                n = g_ref[at, pl.ds(r + 1, 4, stride=9), :]
                n = pltpu.roll(n, 128 - off, axis=1)
                v = jnp.where(lane < 128 - off, v, n)
            r, off = divmod(24 * j, 128)
            k = g_ref[at, pl.ds(36 + r, 4, stride=3), :]
            k = pltpu.roll(k, (72 - off) % 128, axis=1)
            if off + 24 > 128:
                n = g_ref[at, pl.ds(37 + r, 4, stride=3), :]
                n = pltpu.roll(n, (72 - off) % 128, axis=1)
                k = jnp.where(lane < 72 + 128 - off, k, n)
            v = jnp.where(lane < 72, v, jnp.where(lane < 96, k, 0.0))
            t_ref[d, pl.ds(j, 4, stride=16), :] = v
        b = NS * (1, 0, 2)[d]
        v = g_ref[at, 48 : 48 + LIST, :]
        v = pltpu.roll(v, b, axis=1) if b else v
        lists = jnp.where((wide >= b) & (wide < b + NS), v, lists)
    rows = jnp.concatenate([t_ref[0], t_ref[1], t_ref[2]], axis=1)
    r = mm(jnp.concatenate(split(rows, 3), axis=0), p_ref[...])
    r = (r[0:64] + r[64:128]) + r[128:192]
    l_ref[...] = lists
    for h in range(2):
        v = r[:, 128 * h : 128 * h + 128]
        o_ref[h] = v
        lo_ref[32 * h : 32 * h + 32, :] = v[0:32]
        hi_ref[32 * h : 32 * h + 32, :] = v[32:64]
    lo_ref[64 : 64 + LIST, :] = lists
    hi_ref[64 : 64 + LIST, :] = lists


def yslab_kernel(o_ref, l_ref, m_ref, p_ref, la_ref, lo_ref, hi_ref):
    lane = lax.broadcasted_iota(jnp.int32, (LIST, 128), 1)
    first = jnp.where(lane < 48, l_ref[...], pltpu.roll(m_ref[64 : 64 + LIST, :], 48, axis=1))
    second = p_ref[64 : 64 + LIST, :]
    la_ref[0:LIST, :] = first
    la_ref[LIST : 2 * LIST, :] = second
    for out, base in ((lo_ref, 0), (hi_ref, 4)):
        for h in range(2):
            for k in range(4):
                at = 64 * h + 16 * k
                out[at : at + 8, :] = o_ref[h, pl.ds(base + k, 8, stride=8), :]
                out[at + 8 : at + 12, :] = m_ref[pl.ds(32 * h + base + k, 4, stride=8), :]
                out[at + 12 : at + 16, :] = p_ref[pl.ds(32 * h + base + k, 4, stride=8), :]
        out[128 : 128 + LIST, :] = first
        out[128 + LIST : 128 + 2 * LIST, :] = second


def weights_kernel(w2, wl, we, wot, ro, t2, tl, te, to, bo, be, bl, b2, rc):
    def three(w):
        h, l = split(w, 2)
        return jnp.concatenate([h, h, l], axis=1)

    pad = jnp.concatenate([w2[...], jnp.zeros((4, 64), F32)], axis=0)
    t2[...] = three(pad.T)
    tl[...] = three(wl[...].T)
    te[...] = three(we[...].T)
    to[...] = three(wot[...])
    bo[...] = three(wot[...].T)
    be[...] = three(we[...])
    bl[...] = three(wl[...])
    b2[...] = three(w2[4:12, :])
    eye = lax.broadcasted_iota(jnp.int32, (64, 64), 0) == lax.broadcasted_iota(
        jnp.int32, (64, 64), 1
    )
    rc[...] = jnp.sum(jnp.where(eye, jnp.broadcast_to(ro[...], (64, 64)), 0.0), axis=1, keepdims=True)


def poly(x, coefs):
    acc = jnp.full_like(x, coefs[-1])
    for c in coefs[-2::-1]:
        acc = acc * x + c
    return acc


SIN = [math.pi ** (2 * k + 1) * (-1) ** k / math.factorial(2 * k + 1) for k in range(7)]
COS = [math.pi ** (2 * k) * (-1) ** k / math.factorial(2 * k) for k in range(8)]
R3, R5, R15 = math.sqrt(3.0), math.sqrt(5.0), math.sqrt(15.0)
ORDER = (0, 1, 1, 1, 2, 2, 2, 2, 2)


def stack3(v):
    h, l = split(v, 2)
    return jnp.concatenate([h, l, h], axis=0)


def quarter(v):
    return (v[:, 0:128] + v[:, 128:256]) + (v[:, 256:384] + v[:, 384:512])


def four(v):
    return jnp.concatenate([v] * 4, axis=1)


def div(v, k):
    return jnp.floor((v + 0.5) * (1.0 / k))


def cell_of(ce):
    cell = div(ce, 3)
    xy = div(cell, 8)
    x = div(xy, 8)
    return x, xy - 8.0 * x, cell - 8.0 * xy, ce - 3.0 * cell


def table_row(p, q):
    px = jnp.where(p < 4.0, p + 8.0, jnp.where(p < 12.0, p - 4.0, p))
    mid = q - 4.0 + 8.0 * jnp.where(p < 4.0, p + 8.0, jnp.where(p < 12.0, p - 4.0, p))
    return jnp.where(q < 4.0, 128.0 + 16.0 * q + px, jnp.where(q < 12.0, mid, 16.0 * q + px))


def place(x, y, z, atom):
    return (
        x + jnp.where(atom == 1.0, 0.75, 0.25),
        y + jnp.where(atom >= 1.0, 0.75, 0.25),
        z + jnp.where(atom == 2.0, 0.75, 0.25),
    )


def fperm():
    m = np.zeros((128, 128), np.float32)
    for z in range(8):
        for a in range(3):
            for c in range(3):
                m[z * 12 + a * 4 + c, z * 9 + a * 3 + c] = 1.0
    return m


def tiles(of):
    lane = lax.broadcasted_iota(jnp.int32, of, 1)
    row = lax.broadcasted_iota(jnp.int32, of, 0) if of[1] == 128 else lax.shift_right_logical(lane, 7)
    lane = lane & 127
    step = lax.shift_right_logical(row, 1)
    second = row & 1
    dy = jnp.where(step == 0, 0, jnp.where(step == 1, -1, 1))
    dx = jnp.where(second == 1, 1, jnp.where(lane < 48, 0, -1))
    at = jnp.where(lane < 48, lane, lane - 48)
    dz = lax.shift_right_logical(at, 4) - 1
    valid = (row < 6) & (lane < jnp.where(second == 1, 48, 96))
    return [v.astype(F32) for v in (dx, dy, dz)], valid, (row == 0) & (lane >= 16) & (lane < 32), lane


def main_kernel(
    o_ref, la_ref, xm_ref, xp_ref, ym_ref, yp_ref,
    t2, tl, te, to, bo, be, bl, b2, rc, fp_ref,
    en_ref, fo_ref,
    w_s, q_s, g_s, a_s, in_s, dw_s, sc_s, tb_s, ls_s, rk_s, acc_s, out_s, b_s,
):
    halves = []
    for h in range(2):
        v = jnp.concatenate(
            [
                o_ref[h], xm_ref[32 * h : 32 * h + 32, :], xp_ref[32 * h : 32 * h + 32, :],
                ym_ref[64 * h : 64 * h + 64, :], yp_ref[64 * h : 64 * h + 64, :],
            ],
            axis=0,
        )
        halves.append(v.T[0:96])
    tb_s[...] = jnp.concatenate(split(jnp.concatenate(halves, axis=0), 2), axis=0)

    places = [(la_ref, 0), (la_ref, LIST), (ym_ref, 128), (ym_ref, 128 + LIST), (yp_ref, 128), (yp_ref, 128 + LIST)]
    (dx, dy, dz), _, _, _ = tiles((1, 768))
    lst = jnp.concatenate([ref[at : at + LIST, :] for ref, at in places], axis=1)
    high = jnp.floor(lst[0:33] * (1.0 / 64.0))
    low = lst[0:33] - 64.0 * high
    ls_s[...] = jnp.concatenate(
        [
            high[0:32], low[0:32], high[32:33], low[32:33], lst[33:34],
            dx + 1.0, dy + 1.0, dz + 1.0, jnp.zeros((10, 768), F32),
        ],
        axis=0,
    ).astype(BF16)
    (dx, dy, dz), valid, own, lane = tiles((8, 128))
    pad = jnp.zeros((2, 128), F32)
    ce = jnp.concatenate([ref[at + 32 : at + 33, :] for ref, at in places] + [pad], axis=0)
    ct = jnp.concatenate([ref[at + 33 : at + 34, :] for ref, at in places] + [pad], axis=0)
    cx, cy, cz, _ = cell_of(ce)
    flag = valid & (~own) & (ct > 0.0)
    for c, d in ((cx, dx), (cy, dy), (cz, dz)):
        v = c + 8.0 * d
        flag = flag & (v >= -2.0) & (v < 10.0)
    flag = jnp.where(flag, 1.0, 0.0)
    tri = lax.broadcasted_iota(jnp.int32, (128, 128), 0) <= lax.broadcasted_iota(
        jnp.int32, (128, 128), 1
    )
    upto = mm(flag.astype(BF16), jnp.where(tri, 1.0, 0.0).astype(BF16))
    total = jnp.broadcast_to(jnp.sum(flag, axis=1, keepdims=True), (8, 128))
    row = lax.broadcasted_iota(jnp.int32, (8, 128), 0)
    before = jnp.where(row >= 1, pltpu.roll(total, 1, axis=0), 0.0)
    for by in (1, 2, 4):
        before = before + jnp.where(row >= by, pltpu.roll(before, by, axis=0), 0.0)
    rank = jnp.where(flag > 0.0, upto + before + (NS - 1.0), -1.0)
    rk_s[...] = jnp.where(own, (lane - 16).astype(F32), rank)
    ghosts = jnp.sum(flag).astype(jnp.int32)
    blocks = 1 + lax.shift_right_logical(ghosts + (NS - 1), 4)
    acc_s[...] = jnp.zeros((64, 128), F32)
    sc_s[...] = jnp.zeros((8, PAIRS + 128), F32)
    in_s[12:16, :] = jnp.zeros((4, PAIRS), F32)

    apart = lax.broadcasted_iota(jnp.int32, (128, 128), 0) - lax.broadcasted_iota(
        jnp.int32, (128, 128), 1
    )
    comb = jnp.where((apart & 15) == 0, 1.0, 0.0).astype(BF16)

    def slots_sum(v):
        r = mm(jnp.concatenate(split(v, 2), axis=0), comb)
        return r[0:576] + r[576:1152]

    def block(b, carry):
        want = (lax.broadcasted_iota(jnp.int32, (128, 128), 0) & 15) + NS * b
        want = want.astype(F32)
        chosen = jnp.concatenate(
            [jnp.where(want == rk_s[t : t + 1, :], 1.0, 0.0).astype(BF16) for t in range(6)], axis=1
        )
        u = mm(ls_s[...], chosen, ((1,), (1,)))
        sub = lax.broadcasted_iota(jnp.int32, (8, 128), 0)
        mine = sub == lax.shift_right_logical(lax.broadcasted_iota(jnp.int32, (8, 128), 1), 4)

        def slots(at):
            return jnp.concatenate(
                [
                    jnp.sum(jnp.where(mine, u[at + 8 * g : at + 8 * g + 8], 0.0), axis=0, keepdims=True)
                    for g in range(4)
                ],
                axis=1,
            )

        nb = 64.0 * slots(0) + slots(32)
        ce = 64.0 * u[64:65] + u[65:66]
        count = u[66:67]
        shift = [8.0 * (u[67 + k : 68 + k] - 1.0) for k in range(3)]
        cx, cy, cz, ca = cell_of(ce)
        cx, cy, cz = cx + shift[0], cy + shift[1], cz + shift[2]
        pq = div(nb, 36)
        r = nb - 36.0 * pq
        p = div(pq, 12)
        q = pq - 12.0 * p
        s = div(r, 3)
        a = r - 3.0 * s
        p = p + four(shift[0] - 2.0)
        q = q + four(shift[1] - 2.0)
        s = s + four(shift[2] - 2.0)
        lane = lax.broadcasted_iota(jnp.int32, (1, PAIRS), 1)
        alive = lax.shift_right_logical(lane, 4).astype(F32) < four(count)
        live = jnp.where(alive, 1.0, 0.0)
        second = place(p, q, s, a)
        centre = place(cx, cy, cz, ca)
        geo = [second[k] - four(centre[k]) for k in range(3)]
        rows = jnp.concatenate([table_row(p + 4.0, q + 4.0), table_row(cx + 4.0, cy + 4.0)], axis=1)
        rsel = jnp.concatenate([3.0 * (s + 4.0) + a, 3.0 * (cz + 4.0) + ca], axis=1)
        at = lax.broadcasted_iota(jnp.int32, (256, PAIRS + 128), 0).astype(F32)
        hot = jnp.where(at == rows, 1.0, 0.0).astype(BF16)

        got = mm(tb_s[...], hot)
        half = lax.shift_right_logical(
            lax.broadcasted_iota(jnp.int32, (8, PAIRS + 128), 0), 2
        ).astype(F32)
        pick = jnp.zeros((8, PAIRS + 128), F32)
        for k in range(24):
            v = got[8 * k : 8 * k + 8] + got[192 + 8 * k : 200 + 8 * k]
            pick = jnp.where(half + 2.0 * k == rsel, v, pick)
        pick = pick[0:4] + pick[4:8]
        first = four(pick[:, PAIRS:])
        second = pick[:, 0:PAIRS]
        rx = [
            jnp.where(alive, (geo[k] + (second[k : k + 1] - first[k : k + 1])) * CELL, 1.0)
            for k in range(3)
        ]
        d2 = rx[0] * rx[0] + rx[1] * rx[1] + rx[2] * rx[2]
        inv = lax.rsqrt(d2)
        inv = inv * (1.5 - 0.5 * d2 * inv * inv)
        dist = d2 * inv
        ux, uy, uz = [v * inv for v in rx]
        x = dist * (1.0 / CUT)
        inside = x < 1.0
        x = jnp.minimum(x, 1.0)
        x2 = x * x
        x3 = x2 * x
        x5 = x3 * x2
        x6 = x3 * x3
        env = jnp.where(inside, 1.0 + x6 * (-28.0 + x * (48.0 - 21.0 * x)), 0.0)
        denv_dd = jnp.where(inside, (-168.0 / CUT) * x5 * (1.0 - x) * (1.0 - x), 0.0)
        ev = env * live

        n = (lax.broadcasted_iota(jnp.int32, (8, PAIRS), 0) + 1).astype(F32)
        t = n * x
        k = jnp.floor(t + 0.5)
        f = t - k
        sign = 1.0 - 2.0 * (k - 2.0 * jnp.floor(k * 0.5))
        f2 = f * f
        sn = sign * f * poly(f2, SIN)
        cs = sign * poly(f2, COS)
        c0 = math.sqrt(2.0 / CUT)
        sd = sn * (c0 * inv)
        basis = sd * env
        dbasis = (n * cs) * ((c0 * math.pi / CUT) * inv * env) + sd * (denv_dd - env * inv)
        k1, k2 = first[3:4], second[3:4]
        in_s[0:1, :] = jnp.where(k1 == 0.0, 1.0, 0.0)
        in_s[1:2, :] = jnp.where(k1 == 1.0, 1.0, 0.0)
        in_s[2:3, :] = jnp.where(k2 == 0.0, 1.0, 0.0)
        in_s[3:4, :] = jnp.where(k2 == 1.0, 1.0, 0.0)
        in_s[4:12, :] = basis

        def silu(v):
            sg = 1.0 / (1.0 + jnp.exp(-v))
            return v * sg, sg * (1.0 + v * (1.0 - sg))

        h, dh_ = silu(mm(t2[...], stack3(in_s[...])))
        z, dz_ = silu(mm(tl[...], stack3(h)))
        zs = stack3(z)
        e = mm(te[...], zs)
        w_s[...] = e * ev

        ys = [
            None, R3 * ux, R3 * uy, R3 * uz, R15 * ux * uy, R15 * uy * uz,
            (0.5 * R5) * (3.0 * uz * uz - 1.0), R15 * ux * uz, (0.5 * R15) * (ux * ux - uy * uy),
        ]
        yb = [None] + [jnp.broadcast_to(v, (8, PAIRS)) for v in ys[1:]]
        for c in range(8):
            at = slice(8 * c, 8 * c + 8)
            w = w_s[at, :]
            for m in range(9):
                a_s[m, at, :] = 0.2 * quarter(w if m == 0 else w * yb[m])
        a_s[...] = slots_sum(a_s[...].reshape(576, 128)).reshape(9, 64, 128)
        for c in range(8):
            at = slice(8 * c, 8 * c + 8)
            sums = [None, None, None]
            for m in range(9):
                am = four(a_s[m, at, :])
                term = am if m == 0 else yb[m] * am
                l = ORDER[m]
                sums[l] = term if sums[l] is None else sums[l] + term
            for l in range(3):
                q_s[l, at, :] = sums[l]
        wv = w_s[...]
        joined = jnp.concatenate([z] + [wv * q_s[l] for l in range(3)], axis=0)
        y, dy_ = silu(mm(to[...], stack3(joined)))
        ro = rc[...]
        raw = jnp.sum(ro * y, axis=0, keepdims=True)

        @pl.when(b == 0)
        def _():
            en = quarter(raw * ev)
            for by in (16, 32, 64):
                en = en + pltpu.roll(en, by, axis=1)
            en_ref[...] = en[:, 0:NS].reshape(1, 1, NS)

        denv = live * raw
        dj = mm(bo[...], stack3((ro * ev) * dy_))
        g_s[...] = dj[64:256]
        for c in range(8):
            at = slice(8 * c, 8 * c + 8)
            w = w_s[at, :]
            for l in range(3):
                gw = g_s[64 * l + 8 * c : 64 * l + 8 * c + 8, :] * w
                for m in range(9):
                    if ORDER[m] == l:
                        b_s[m, at, :] = 0.2 * quarter(gw if m == 0 else gw * yb[m])
        b_s[...] = slots_sum(b_s[...].reshape(576, 128)).reshape(9, 64, 128)
        acc = [None] * 9
        for c in range(8):
            at = slice(8 * c, 8 * c + 8)
            w = w_s[at, :]
            dw = None
            for l in range(3):
                g = g_s[64 * l + 8 * c : 64 * l + 8 * c + 8, :]
                part = g * q_s[l, at, :]
                dw = part if dw is None else dw + part
                gw = g * w
                for m in range(9):
                    if ORDER[m] != l:
                        continue
                    bm = four(b_s[m, at, :])
                    dw = dw + (bm if m == 0 else yb[m] * bm)
                    if m:
                        v = gw * four(a_s[m, at, :]) + w * bm
                        acc[m] = v if acc[m] is None else acc[m] + v
            dw_s[at, :] = dw
        dw = dw_s[...]
        denv = denv + live * jnp.sum(dw * e, axis=0, keepdims=True)
        dz = dj[0:64] + mm(be[...], stack3(dw * ev))
        dh = mm(bl[...], stack3(dz * dz_))
        db = mm(b2[...], stack3(dh * dh_))
        dd = denv * denv_dd + jnp.sum(db * dbasis, axis=0, keepdims=True)
        dy = [None] + [jnp.sum(acc[m], axis=0, keepdims=True) for m in range(1, 9)]
        du0 = R3 * dy[1] + R15 * (uy * dy[4] + uz * dy[7] + ux * dy[8])
        du1 = R3 * dy[2] + R15 * (ux * dy[4] + uz * dy[5] - uy * dy[8])
        du2 = R3 * dy[3] + R15 * (uy * dy[5] + ux * dy[7]) + (3.0 * R5) * uz * dy[6]
        along = ux * du0 + uy * du1 + uz * du2
        dd = dd - along * inv
        grad = [du0 * inv + ux * dd, du1 * inv + uy * dd, du2 * inv + uz * dd]
        for k in range(3):
            mine = quarter(grad[k])
            for row in (k, k + 4):
                sc_s[row : row + 1, 0:PAIRS] = -grad[k]
                sc_s[row : row + 1, PAIRS:] = mine
        gv = sc_s[...]
        m = jnp.concatenate(
            [jnp.where(half + (12.0 + 2.0 * k) == rsel, gv, 0.0) for k in range(12)]
            + [jnp.zeros((32, PAIRS + 128), F32)],
            axis=0,
        )
        mh, ml = split(m, 2)
        nt = ((1,), (1,))
        acc_s[...] += mm(hot[0:64], mh, nt) + mm(hot[0:64], ml, nt)
        return carry

    lax.fori_loop(0, blocks, block, 0)

    r = mm(jnp.concatenate(split(acc_s[...], 3), axis=0), fp_ref[...])
    out_s[...] = (r[0:64] + r[64:128]) + r[128:192]
    lane = lax.broadcasted_iota(jnp.int32, (4, 128), 1)
    for k in range(9):
        v = jnp.zeros((4, 128), F32)
        for j in range(128 * k // 72, (128 * k + 127) // 72 + 1):
            off = 72 * j - 128 * k
            part = pltpu.roll(out_s[pl.ds(j, 4, stride=16), :], off % 128, axis=1)
            v = v + jnp.where((lane >= off) & (lane < off + 72), part, 0.0)
        for g in range(4):
            fo_ref[0, :, 128 * (9 * g + k) : 128 * (9 * g + k) + 128] = v[g : g + 1]


def sds(shape, dtype=F32):
    return jax.ShapeDtypeStruct(shape, dtype)


def hop(v, axis, by):
    n = lax.axis_size(axis)
    return lax.ppermute(v, axis, [(i, (i + by) % n) for i in range(n)])


def local(
    displacement, species, centres, neighbours, neighbour_count, live_centres,
    w_two, w_lat, w_env, w_out, readout,
):
    e = lax.axis_index("gz").astype(jnp.int32).reshape(1)
    flat = call(
        pack_kernel,
        sds((48 + LIST, 128)),
        [
            (pltpu.with_memory_space_constraint(v, pltpu.HBM), HB)
            for v in (displacement, species, neighbours, centres, neighbour_count)
        ]
        + [(live_centres.reshape(1), SM)],
        "pack",
        [
            pltpu.VMEM((128, 128), F32), pltpu.VMEM((1, 1, 4608), F32),
            pltpu.VMEM((1, 1, 1536), jnp.int32), pltpu.VMEM((1, 1, 512), jnp.int32),
            pltpu.VMEM((1, 1, NS), jnp.int32), pltpu.VMEM((1, 1, NS), jnp.int32),
            pltpu.SemaphoreType.DMA((5,)),
        ],
    )
    column = lax.all_gather(flat, "gz")
    slab = sds((64 + LIST, 128))
    own, lists, lo, hi = call(
        zrows_kernel,
        (sds((2, 64, 128)), sds((LIST, 128)), slab, slab),
        [(e, SM), (column, VM), (jnp.asarray(zperm(), BF16), VM)],
        "zrows",
        [pltpu.VMEM((3, 64, 128), F32)],
    )
    xm, xp = hop(hi, "gx", 1), hop(lo, "gx", -1)
    ws = call(
        weights_kernel,
        (
            sds((64, 48), BF16), sds((64, 192), BF16), sds((64, 192), BF16), sds((64, 768), BF16),
            sds((256, 192), BF16), sds((64, 192), BF16), sds((64, 192), BF16), sds((8, 192), BF16),
            sds((64, 1)),
        ),
        [(v, VM) for v in (w_two, w_lat, w_env, w_out.T, readout.reshape(1, 64))],
        "weights",
    )
    slab = sds((128 + 2 * LIST, 128))
    lists, lo, hi = call(
        yslab_kernel,
        (sds((2 * LIST, 128)), slab, slab),
        [(v, VM) for v in (own, lists, xm, xp)],
        "yslab",
    )
    ym, yp = hop(hi, "gy", 1), hop(lo, "gy", -1)
    return call(
        main_kernel,
        (sds((1, 1, NS)), sds((1, 1, 4608))),
        [(v, VM) for v in (own, lists, xm, xp, ym, yp, *ws, jnp.asarray(fperm(), BF16))],
        "pairs",
        [
            pltpu.VMEM((64, PAIRS), F32), pltpu.VMEM((3, 64, PAIRS), F32),
            pltpu.VMEM((192, PAIRS), F32), pltpu.VMEM((9, 64, 128), F32),
            pltpu.VMEM((16, PAIRS), F32), pltpu.VMEM((64, PAIRS), F32),
            pltpu.VMEM((8, PAIRS + 128), F32), pltpu.VMEM((384, 256), BF16),
            pltpu.VMEM((80, 768), BF16), pltpu.VMEM((8, 128), F32),
            pltpu.VMEM((64, 128), F32), pltpu.VMEM((64, 128), F32),
            pltpu.VMEM((9, 64, 128), F32),
        ],
        mib=16,
    )


def solution(mesh):
    cut = P("gx", "gy", "gz")
    return jax.shard_map(
        local,
        mesh=mesh,
        in_specs=(cut,) * 6 + (P(),) * 5,
        out_specs=(cut, cut),
        check_vma=False,
    )
```

profile of v0, /device:TPU:16, one launch (start us, length us, event | category | flops | bytes accessed | tf_op | source)
XLA Modules:
  0.0 59.7 jit_solution(6545475364725992855)
XLA Ops:
  0.6 0.0 copy-start
  1.3 0.9 %pack.1 = f32[88,128]{1,0:T(8,128)S(1)} custom-call(f32[1,1,4608]{2,1,0:T(1,128)} %d_in.1, s32[1,1,1536]{2,1,0:T(1,128)} %s_in.1, s32[1,1,512]{2,1,0:T(1,128)} %nb_in.1, s32[1,1,16]{2,1,0:T(1,128)} %ce_in.1, s32[1,1,16]{2,1,0:T(1,128)} %ct_in.1, s32[1]{0:T(128)} %bitcast.5.al_ref), custom_call_target="tpu_custom_call" | custom-call | tf_op jit(solution)/shard_map/pack/pallas_call | solution.py:25
  2.3 17.0 %all-gather = f32[352,128]{1,0:T(8,128)S(1)} all-gather(f32[88,128]{1,0:T(8,128)S(1)} %pack.1), channel_id=2, replica_groups=mesh['gx'=32,'gy'=8,'gz'=4] {'gz'}, dimensions={0}, use_global_device_ids=true | all-gather | bytes 225280 | tf_op jit(solution)/shard_map/all_gather | solution.py:551
  19.3 0.0 copy-done
  19.3 0.4 zrows.1
  19.7 1.9 %collective-permute-start = (f32[104,128]{1,0:T(8,128)S(1)}, f32[104,128]{1,0:T(8,128)S(1)}, u32[]{:S(2)}, u32[]{:S(2)}) collective-permute-start(f32[104,128]{1,0:T(8,128)S(1)} %get-tuple-element.20), channel_id=1, source_target_pairs={{0,32},{32,64},{64,96},{96,128},{128,160},{160,192},{192,224},{224... | collective-permute-start | bytes 159752 | tf_op jit(solution)/shard_map/ppermute | solution.py:527
  21.6 8.1 %collective-permute-start.1 = (f32[104,128]{1,0:T(8,128)S(1)}, f32[104,128]{1,0:T(8,128)S(1)}, u32[]{:S(2)}, u32[]{:S(2)}) collective-permute-start(f32[104,128]{1,0:T(8,128)S(1)} %get-tuple-element.21), channel_id=1, source_target_pairs={{0,992},{32,0},{64,32},{96,64},{128,96},{160,128},{192,160},{224,1... | collective-permute-start | bytes 159752 | tf_op jit(solution)/shard_map/ppermute | solution.py:527
  29.8 0.4 collective-permute-done.m_ref.xm_ref
  30.2 1.3 %collective-permute-done.1.p_ref.xp_ref = f32[104,128]{1,0:T(8,128)S(1)} collective-permute-done((f32[104,128]{1,0:T(8,128)S(1)}, f32[104,128]{1,0:T(8,128)S(1)}, u32[]{:S(2)}, u32[]{:S(2)}) %collective-permute-start.1) | collective-permute-done | bytes 53280 | tf_op jit(solution)/shard_map/ppermute | solution.py:527
  31.5 0.0 copy-start.1
  31.5 0.0 copy-start.2
  31.5 0.0 copy-start.3
  31.5 0.0 copy-start.5
  31.5 0.1 yslab.1
  31.6 1.9 %collective-permute-start.2 = (f32[208,128]{1,0:T(8,128)S(1)}, f32[208,128]{1,0:T(8,128)S(1)}, u32[]{:S(2)}, u32[]{:S(2)}) collective-permute-start(f32[208,128]{1,0:T(8,128)S(1)} %get-tuple-element.23), channel_id=1, source_target_pairs={{0,4},{4,8},{8,12},{12,16},{16,20},{20,24},{24,28},{28,0},{1,5},{5... | collective-permute-start | bytes 319496 | tf_op jit(solution)/shard_map/ppermute | solution.py:527
  33.5 6.0 %collective-permute-start.3 = (f32[208,128]{1,0:T(8,128)S(1)}, f32[208,128]{1,0:T(8,128)S(1)}, u32[]{:S(2)}, u32[]{:S(2)}) collective-permute-start(f32[208,128]{1,0:T(8,128)S(1)} %get-tuple-element.24), channel_id=1, source_target_pairs={{0,28},{4,0},{8,4},{12,8},{16,12},{20,16},{24,20},{28,24},{1,29},{... | collective-permute-start | bytes 319496 | tf_op jit(solution)/shard_map/ppermute | solution.py:527
  39.5 0.0 copy-start.6
  39.5 0.0 copy-done.1
  39.5 0.0 copy-done.2
  39.5 0.0 copy-done.3
  39.6 0.0 copy-done.5
  39.6 0.6 %copy-done.6 = f32[64]{0:T(128)S(1)} copy-done((f32[64]{0:T(128)S(1)}, f32[64]{0:T(128)}, u32[]{:S(2)}) %copy-start.6) | copy-done | bytes 280
  40.2 0.0 copy-start.4
  40.2 0.2 weights.1
  40.4 0.0 collective-permute-done.2.ym_ref
  40.4 1.4 %collective-permute-done.3.yp_ref = f32[208,128]{1,0:T(8,128)S(1)} collective-permute-done((f32[208,128]{1,0:T(8,128)S(1)}, f32[208,128]{1,0:T(8,128)S(1)}, u32[]{:S(2)}, u32[]{:S(2)}) %collective-permute-start.3) | collective-permute-done | bytes 106528 | tf_op jit(solution)/shard_map/ppermute | solution.py:527
  41.8 0.0 copy-done.4
  41.8 17.9 %pairs.1 = (f32[1,1,16]{2,1,0:T(1,128)}, f32[1,1,4608]{2,1,0:T(1,128)}) custom-call(f32[2,64,128]{2,1,0:T(8,128)S(1)} %get-tuple-element.18.o_ref, f32[80,128]{1,0:T(8,128)S(1)} %get-tuple-element.22.la_ref, f32[104,128]{1,0:T(8,128)S(1)} %collective-permute-done.m_ref.xm_ref, f32[104,128]{1,0:T(8,128)S(1)} %collective-permute-done.1.p_ref.xp_ref, ...), custom_call_target="tpu_custom_call" | custom-call | tf_op jit(solution)/shard_map/pairs/pallas_call | solution.py:25
Async XLA Ops:
  0.6 18.7 %copy-start = (bf16[384,256]{1,0:T(8,128)(2,1)S(1)}, bf16[384,256]{1,0:T(8,128)(2,1)}, u32[]{:S(2)}) copy-start(bf16[384,256]{1,0:T(8,128)(2,1)} %constant.8.clone.p_ref) | copy-start | bytes 589828
  19.7 10.5 %collective-permute-start = (f32[104,128]{1,0:T(8,128)S(1)}, f32[104,128]{1,0:T(8,128)S(1)}, u32[]{:S(2)}, u32[]{:S(2)}) collective-permute-start(f32[104,128]{1,0:T(8,128)S(1)} %get-tuple-element.20), channel_id=1, source_target_pairs={{0,32},{32,64},{64,96},{96,128},{128,160},{160,192},{192,224},{224... | collective-permute-start | bytes 159752 | tf_op jit(solution)/shard_map/ppermute | solution.py:527
  21.6 9.9 %collective-permute-start.1 = (f32[104,128]{1,0:T(8,128)S(1)}, f32[104,128]{1,0:T(8,128)S(1)}, u32[]{:S(2)}, u32[]{:S(2)}) collective-permute-start(f32[104,128]{1,0:T(8,128)S(1)} %get-tuple-element.21), channel_id=1, source_target_pairs={{0,992},{32,0},{64,32},{96,64},{128,96},{160,128},{192,160},{224,1... | collective-permute-start | bytes 159752 | tf_op jit(solution)/shard_map/ppermute | solution.py:527
  31.5 8.0 %copy-start.1 = (f32[256,64]{0,1:T(8,128)S(1)}, f32[256,64]{0,1:T(8,128)}, u32[]{:S(2)}) copy-start(f32[256,64]{0,1:T(8,128)} %param.22) | copy-start | bytes 196612
  31.5 8.0 %copy-start.2 = (f32[64,64]{1,0:T(8,128)S(1)}, f32[64,64]{1,0:T(8,128)}, u32[]{:S(2)}) copy-start(f32[64,64]{1,0:T(8,128)} %wl.1) | copy-start | bytes 49156
  31.5 8.0 %copy-start.3 = (f32[64,64]{1,0:T(8,128)S(1)}, f32[64,64]{1,0:T(8,128)}, u32[]{:S(2)}) copy-start(f32[64,64]{1,0:T(8,128)} %we.1) | copy-start | bytes 49156
  31.5 8.0 %copy-start.5 = (f32[12,64]{1,0:T(8,128)S(1)}, f32[12,64]{1,0:T(8,128)}, u32[]{:S(2)}) copy-start(f32[12,64]{1,0:T(8,128)} %w2.1) | copy-start | bytes 9220
  31.6 8.8 %collective-permute-start.2 = (f32[208,128]{1,0:T(8,128)S(1)}, f32[208,128]{1,0:T(8,128)S(1)}, u32[]{:S(2)}, u32[]{:S(2)}) collective-permute-start(f32[208,128]{1,0:T(8,128)S(1)} %get-tuple-element.23), channel_id=1, source_target_pairs={{0,4},{4,8},{8,12},{12,16},{16,20},{20,24},{24,28},{28,0},{1,5},{5... | collective-permute-start | bytes 319496 | tf_op jit(solution)/shard_map/ppermute | solution.py:527
  33.5 8.2 %collective-permute-start.3 = (f32[208,128]{1,0:T(8,128)S(1)}, f32[208,128]{1,0:T(8,128)S(1)}, u32[]{:S(2)}, u32[]{:S(2)}) collective-permute-start(f32[208,128]{1,0:T(8,128)S(1)} %get-tuple-element.24), channel_id=1, source_target_pairs={{0,28},{4,0},{8,4},{12,8},{16,12},{20,16},{24,20},{28,24},{1,29},{... | collective-permute-start | bytes 319496 | tf_op jit(solution)/shard_map/ppermute | solution.py:527
  39.5 0.7 %copy-start.6 = (f32[64]{0:T(128)S(1)}, f32[64]{0:T(128)}, u32[]{:S(2)}) copy-start(f32[64]{0:T(128)} %param.23) | copy-start | bytes 772
  40.2 1.6 %copy-start.4 = (bf16[128,128]{1,0:T(8,128)(2,1)S(1)}, bf16[128,128]{1,0:T(8,128)(2,1)}, u32[]{:S(2)}) copy-start(bf16[128,128]{1,0:T(8,128)(2,1)} %constant.9.clone.fp_ref) | copy-start | bytes 98308
where the time goes:
time: 59.2 us; the launch traced here: 59.7 us
  Pallas kernels  19.5 us (33%)
  starting transfers between devices  17.9 us (30%)
  blocking collectives  17 us (29%)
  waiting for transfers between devices  3.13 us (5%)
  between operations  1.44 us (2%)
  local copies, waits for them, and re-layouts  0.64 us (1%)
    pallas_call x5, Pallas kernels, call(): pl.pallas_call(kernel, out_shape=outs, in_specs=specs, out_specs=jax.tree...  19.5 us
    ppermute x4, starting transfers between devices, hop(): return lax.ppermute(v, axis, [(i, (i + by) % n) for i in range(n)])  17.9 us
    all_gather x1, blocking collectives, local(): column = lax.all_gather(flat, 'gz')  17 us
    ppermute x4, waiting for transfers between devices, hop(): return lax.ppermute(v, axis, [(i, (i + by) % n) for i in range(n)])  3.13 us
  transfers between devices with their start and end apart: 4, of which 3 were waited for; matrix products, arithmetic and copies ran while one was open for 0% of the time, Pallas kernels for 0%

commit v1 on v0

--- a/solution.py
+++ b/solution.py
@@ -15,8 +15,10 @@
 VM = pl.BlockSpec(memory_space=pltpu.VMEM)
 SM = pl.BlockSpec(memory_space=pltpu.SMEM)
 HB = pl.BlockSpec(memory_space=pltpu.HBM)
-PAIRS = 512
 NS = 16
+NB = 64
+PAIRS = 32 * NB
+TILES = PAIRS // 128
 LIST = 40
 
 
@@ -182,12 +184,15 @@
     return jnp.concatenate([h, l, h], axis=0)
 
 
-def quarter(v):
-    return (v[:, 0:128] + v[:, 128:256]) + (v[:, 256:384] + v[:, 384:512])
-
-
-def four(v):
-    return jnp.concatenate([v] * 4, axis=1)
+def fold(v):
+    parts = [v[:, 128 * i : 128 * i + 128] for i in range(TILES)]
+    while len(parts) > 1:
+        parts = [a + b for a, b in zip(parts[0::2], parts[1::2])]
+    return parts[0]
+
+
+def wide(v):
+    return jnp.concatenate([v] * TILES, axis=1)
 
 
 def div(v, k):
@@ -287,10 +292,11 @@
     before = jnp.where(row >= 1, pltpu.roll(total, 1, axis=0), 0.0)
     for by in (1, 2, 4):
         before = before + jnp.where(row >= by, pltpu.roll(before, by, axis=0), 0.0)
-    rank = jnp.where(flag > 0.0, upto + before + (NS - 1.0), -1.0)
-    rk_s[...] = jnp.where(own, (lane - 16).astype(F32), rank)
-    ghosts = jnp.sum(flag).astype(jnp.int32)
-    blocks = 1 + lax.shift_right_logical(ghosts + (NS - 1), 4)
+    mine = own & (ct > 0.0)
+    owned = jnp.sum(jnp.where(mine, 1.0, 0.0))
+    rank = jnp.where(flag > 0.0, upto + before + (owned - 1.0), -1.0)
+    rk_s[...] = jnp.where(mine, (lane - 16).astype(F32), rank)
+    blocks = lax.div((owned + jnp.sum(flag)).astype(jnp.int32) + (NB - 1), NB)
     acc_s[...] = jnp.zeros((64, 128), F32)
     sc_s[...] = jnp.zeros((8, PAIRS + 128), F32)
     in_s[12:16, :] = jnp.zeros((4, PAIRS), F32)
@@ -298,27 +304,26 @@
     apart = lax.broadcasted_iota(jnp.int32, (128, 128), 0) - lax.broadcasted_iota(
         jnp.int32, (128, 128), 1
     )
-    comb = jnp.where((apart & 15) == 0, 1.0, 0.0).astype(BF16)
+    comb = jnp.where((apart & (NB - 1)) == 0, 1.0, 0.0).astype(BF16)
 
     def slots_sum(v):
         r = mm(jnp.concatenate(split(v, 2), axis=0), comb)
         return r[0:576] + r[576:1152]
 
     def block(b, carry):
-        want = (lax.broadcasted_iota(jnp.int32, (128, 128), 0) & 15) + NS * b
+        want = (lax.broadcasted_iota(jnp.int32, (128, 128), 0) & (NB - 1)) + NB * b
         want = want.astype(F32)
         chosen = jnp.concatenate(
             [jnp.where(want == rk_s[t : t + 1, :], 1.0, 0.0).astype(BF16) for t in range(6)], axis=1
         )
         u = mm(ls_s[...], chosen, ((1,), (1,)))
-        sub = lax.broadcasted_iota(jnp.int32, (8, 128), 0)
-        mine = sub == lax.shift_right_logical(lax.broadcasted_iota(jnp.int32, (8, 128), 1), 4)
+        left = lax.broadcasted_iota(jnp.int32, (1, 128), 1) < NB
 
         def slots(at):
             return jnp.concatenate(
                 [
-                    jnp.sum(jnp.where(mine, u[at + 8 * g : at + 8 * g + 8], 0.0), axis=0, keepdims=True)
-                    for g in range(4)
+                    jnp.where(left, u[at + 2 * g : at + 2 * g + 1], u[at + 2 * g + 1 : at + 2 * g + 2])
+                    for g in range(TILES)
                 ],
                 axis=1,
             )
@@ -335,15 +340,15 @@
         q = pq - 12.0 * p
         s = div(r, 3)
         a = r - 3.0 * s
-        p = p + four(shift[0] - 2.0)
-        q = q + four(shift[1] - 2.0)
-        s = s + four(shift[2] - 2.0)
+        p = p + wide(shift[0] - 2.0)
+        q = q + wide(shift[1] - 2.0)
+        s = s + wide(shift[2] - 2.0)
         lane = lax.broadcasted_iota(jnp.int32, (1, PAIRS), 1)
-        alive = lax.shift_right_logical(lane, 4).astype(F32) < four(count)
+        alive = lax.div(lane, NB).astype(F32) < wide(count)
         live = jnp.where(alive, 1.0, 0.0)
         second = place(p, q, s, a)
         centre = place(cx, cy, cz, ca)
-        geo = [second[k] - four(centre[k]) for k in range(3)]
+        geo = [second[k] - wide(centre[k]) for k in range(3)]
         rows = jnp.concatenate([table_row(p + 4.0, q + 4.0), table_row(cx + 4.0, cy + 4.0)], axis=1)
         rsel = jnp.concatenate([3.0 * (s + 4.0) + a, 3.0 * (cz + 4.0) + ca], axis=1)
         at = lax.broadcasted_iota(jnp.int32, (256, PAIRS + 128), 0).astype(F32)
@@ -358,7 +363,7 @@
             v = got[8 * k : 8 * k + 8] + got[192 + 8 * k : 200 + 8 * k]
             pick = jnp.where(half + 2.0 * k == rsel, v, pick)
         pick = pick[0:4] + pick[4:8]
-        first = four(pick[:, PAIRS:])
+        first = wide(pick[:, PAIRS:])
         second = pick[:, 0:PAIRS]
         rx = [
             jnp.where(alive, (geo[k] + (second[k : k + 1] - first[k : k + 1])) * CELL, 1.0)
@@ -400,7 +405,7 @@
         in_s[4:12, :] = basis
 
         def silu(v):
-            sg = 1.0 / (1.0 + jnp.exp(-v))
+            sg = 0.5 + 0.5 * jnp.tanh(0.5 * v)
             return v * sg, sg * (1.0 + v * (1.0 - sg))
 
         h, dh_ = silu(mm(t2[...], stack3(in_s[...])))
@@ -418,13 +423,13 @@
             at = slice(8 * c, 8 * c + 8)
             w = w_s[at, :]
             for m in range(9):
-                a_s[m, at, :] = 0.2 * quarter(w if m == 0 else w * yb[m])
+                a_s[m, at, :] = 0.2 * fold(w if m == 0 else w * yb[m])
         a_s[...] = slots_sum(a_s[...].reshape(576, 128)).reshape(9, 64, 128)
         for c in range(8):
             at = slice(8 * c, 8 * c + 8)
             sums = [None, None, None]
             for m in range(9):
-                am = four(a_s[m, at, :])
+                am = wide(a_s[m, at, :])
                 term = am if m == 0 else yb[m] * am
                 l = ORDER[m]
                 sums[l] = term if sums[l] is None else sums[l] + term
@@ -438,9 +443,10 @@
 
         @pl.when(b == 0)
         def _():
-            en = quarter(raw * ev)
-            for by in (16, 32, 64):
-                en = en + pltpu.roll(en, by, axis=1)
+            en = fold(raw * ev)
+            en = en + pltpu.roll(en, NB, axis=1)
+            first_lanes = lax.broadcasted_iota(jnp.int32, (1, 128), 1).astype(F32)
+            en = jnp.where(first_lanes < owned, en, 0.0)
             en_ref[...] = en[:, 0:NS].reshape(1, 1, NS)
 
         denv = live * raw
@@ -453,7 +459,7 @@
                 gw = g_s[64 * l + 8 * c : 64 * l + 8 * c + 8, :] * w
                 for m in range(9):
                     if ORDER[m] == l:
-                        b_s[m, at, :] = 0.2 * quarter(gw if m == 0 else gw * yb[m])
+                        b_s[m, at, :] = 0.2 * fold(gw if m == 0 else gw * yb[m])
         b_s[...] = slots_sum(b_s[...].reshape(576, 128)).reshape(9, 64, 128)
         acc = [None] * 9
         for c in range(8):
@@ -468,10 +474,10 @@
                 for m in range(9):
                     if ORDER[m] != l:
                         continue
-                    bm = four(b_s[m, at, :])
+                    bm = wide(b_s[m, at, :])
                     dw = dw + (bm if m == 0 else yb[m] * bm)
                     if m:
-                        v = gw * four(a_s[m, at, :]) + w * bm
+                        v = gw * wide(a_s[m, at, :]) + w * bm
                         acc[m] = v if acc[m] is None else acc[m] + v
             dw_s[at, :] = dw
         dw = dw_s[...]
@@ -488,7 +494,7 @@
         dd = dd - along * inv
         grad = [du0 * inv + ux * dd, du1 * inv + uy * dd, du2 * inv + uz * dd]
         for k in range(3):
-            mine = quarter(grad[k])
+            mine = fold(grad[k])
             for row in (k, k + 4):
                 sc_s[row : row + 1, 0:PAIRS] = -grad[k]
                 sc_s[row : row + 1, PAIRS:] = mine
@@ -590,7 +596,7 @@
             pltpu.VMEM((64, 128), F32), pltpu.VMEM((64, 128), F32),
             pltpu.VMEM((9, 64, 128), F32),
         ],
-        mib=16,
+        mib=24,
     )
 
 

time: 59.2 us -> 54.1 us (0.914)
  the two profiles are of different devices: /device:TPU:16 before, /device:TPU:46 now
where the time goes in v1:
time: 54.1 us; the launch traced here: 53.8 us
  starting transfers between devices  26.9 us (50%)
  waiting for transfers between devices  10.1 us (19%)
  Pallas kernels  9.15 us (17%)
  blocking collectives  5.55 us (10%)
  between operations  1.45 us (3%)
  local copies, waits for them, and re-layouts  0.64 us (1%)
    ppermute x4, starting transfers between devices, hop(): return lax.ppermute(v, axis, [(i, (i + by) % n) for i in range(n)])  26.9 us
    ppermute x4, waiting for transfers between devices, hop(): return lax.ppermute(v, axis, [(i, (i + by) % n) for i in range(n)])  10.1 us
    pallas_call x5, Pallas kernels, call(): pl.pallas_call(kernel, out_shape=outs, in_specs=specs, out_specs=jax.tree...  9.15 us
    all_gather x1, blocking collectives, local(): column = lax.all_gather(flat, 'gz')  5.55 us
  transfers between devices with their start and end apart: 4, of which 2 were waited for; matrix products, arithmetic and copies ran while one was open for 0% of the time, Pallas kernels for 0%

profile of v1, /device:TPU:46, one launch (start us, length us, event | category | flops | bytes accessed | tf_op | source)
XLA Modules:
  0.0 53.8 jit_solution(2863137191549288700)
XLA Ops:
  0.6 0.0 copy-start
  1.3 0.9 %pack.1 = f32[88,128]{1,0:T(8,128)S(1)} custom-call(f32[1,1,4608]{2,1,0:T(1,128)} %d_in.1, s32[1,1,1536]{2,1,0:T(1,128)} %s_in.1, s32[1,1,512]{2,1,0:T(1,128)} %nb_in.1, s32[1,1,16]{2,1,0:T(1,128)} %ce_in.1, s32[1,1,16]{2,1,0:T(1,128)} %ct_in.1, s32[1]{0:T(128)} %bitcast.5.al_ref), custom_call_target="tpu_custom_call" | custom-call | tf_op jit(solution)/shard_map/pack/pallas_call | solution.py:27
  2.3 5.6 %all-gather = f32[352,128]{1,0:T(8,128)S(1)} all-gather(f32[88,128]{1,0:T(8,128)S(1)} %pack.1), channel_id=2, replica_groups=mesh['gx'=32,'gy'=8,'gz'=4] {'gz'}, dimensions={0}, use_global_device_ids=true | all-gather | bytes 225280 | tf_op jit(solution)/shard_map/all_gather | solution.py:557
  7.8 0.0 copy-done
  7.8 0.4 zrows.1
  8.2 5.7 %collective-permute-start = (f32[104,128]{1,0:T(8,128)S(1)}, f32[104,128]{1,0:T(8,128)S(1)}, u32[]{:S(2)}, u32[]{:S(2)}) collective-permute-start(f32[104,128]{1,0:T(8,128)S(1)} %get-tuple-element.20), channel_id=1, source_target_pairs={{0,32},{32,64},{64,96},{96,128},{128,160},{160,192},{192,224},{224... | collective-permute-start | bytes 159752 | tf_op jit(solution)/shard_map/ppermute | solution.py:533
  14.0 1.9 %collective-permute-start.1 = (f32[104,128]{1,0:T(8,128)S(1)}, f32[104,128]{1,0:T(8,128)S(1)}, u32[]{:S(2)}, u32[]{:S(2)}) collective-permute-start(f32[104,128]{1,0:T(8,128)S(1)} %get-tuple-element.21), channel_id=1, source_target_pairs={{0,992},{32,0},{64,32},{96,64},{128,96},{160,128},{192,160},{224,1... | collective-permute-start | bytes 159752 | tf_op jit(solution)/shard_map/ppermute | solution.py:533
  15.9 0.0 collective-permute-done.m_ref.xm_ref
  15.9 8.8 %collective-permute-done.1.p_ref.xp_ref = f32[104,128]{1,0:T(8,128)S(1)} collective-permute-done((f32[104,128]{1,0:T(8,128)S(1)}, f32[104,128]{1,0:T(8,128)S(1)}, u32[]{:S(2)}, u32[]{:S(2)}) %collective-permute-start.1) | collective-permute-done | bytes 53280 | tf_op jit(solution)/shard_map/ppermute | solution.py:533
  24.7 0.0 copy-start.1
  24.7 0.0 copy-start.2
  24.7 0.0 copy-start.3
  24.7 0.0 copy-start.5
  24.7 0.1 yslab.1
  24.8 5.2 %collective-permute-start.2 = (f32[208,128]{1,0:T(8,128)S(1)}, f32[208,128]{1,0:T(8,128)S(1)}, u32[]{:S(2)}, u32[]{:S(2)}) collective-permute-start(f32[208,128]{1,0:T(8,128)S(1)} %get-tuple-element.23), channel_id=1, source_target_pairs={{0,4},{4,8},{8,12},{12,16},{16,20},{20,24},{24,28},{28,0},{1,5},{5... | collective-permute-start | bytes 319496 | tf_op jit(solution)/shard_map/ppermute | solution.py:533
  29.9 14.0 %collective-permute-start.3 = (f32[208,128]{1,0:T(8,128)S(1)}, f32[208,128]{1,0:T(8,128)S(1)}, u32[]{:S(2)}, u32[]{:S(2)}) collective-permute-start(f32[208,128]{1,0:T(8,128)S(1)} %get-tuple-element.24), channel_id=1, source_target_pairs={{0,28},{4,0},{8,4},{12,8},{16,12},{20,16},{24,20},{28,24},{1,29},{... | collective-permute-start | bytes 319496 | tf_op jit(solution)/shard_map/ppermute | solution.py:533
  44.0 0.0 copy-start.6
  44.0 0.0 copy-done.1
  44.0 0.0 copy-done.2
  44.0 0.0 copy-done.3
  44.0 0.0 copy-done.5
  44.1 0.6 %copy-done.6 = f32[64]{0:T(128)S(1)} copy-done((f32[64]{0:T(128)S(1)}, f32[64]{0:T(128)}, u32[]{:S(2)}) %copy-start.6) | copy-done | bytes 280
  44.7 0.0 copy-start.4
  44.7 0.2 weights.1
  44.9 0.0 collective-permute-done.2.ym_ref
  44.9 1.4 %collective-permute-done.3.yp_ref = f32[208,128]{1,0:T(8,128)S(1)} collective-permute-done((f32[208,128]{1,0:T(8,128)S(1)}, f32[208,128]{1,0:T(8,128)S(1)}, u32[]{:S(2)}, u32[]{:S(2)}) %collective-permute-start.3) | collective-permute-done | bytes 106528 | tf_op jit(solution)/shard_map/ppermute | solution.py:533
  46.3 0.0 copy-done.4
  46.3 7.5 %pairs.1 = (f32[1,1,16]{2,1,0:T(1,128)}, f32[1,1,4608]{2,1,0:T(1,128)}) custom-call(f32[2,64,128]{2,1,0:T(8,128)S(1)} %get-tuple-element.18.o_ref, f32[80,128]{1,0:T(8,128)S(1)} %get-tuple-element.22.la_ref, f32[104,128]{1,0:T(8,128)S(1)} %collective-permute-done.m_ref.xm_ref, f32[104,128]{1,0:T(8,128)S(1)} %collective-permute-done.1.p_ref.xp_ref, ...), custom_call_target="tpu_custom_call" | custom-call | tf_op jit(solution)/shard_map/pairs/pallas_call | solution.py:27
Async XLA Ops:
  0.6 7.2 %copy-start = (bf16[384,256]{1,0:T(8,128)(2,1)S(1)}, bf16[384,256]{1,0:T(8,128)(2,1)}, u32[]{:S(2)}) copy-start(bf16[384,256]{1,0:T(8,128)(2,1)} %constant.8.clone.p_ref) | copy-start | bytes 589828
  8.2 7.7 %collective-permute-start = (f32[104,128]{1,0:T(8,128)S(1)}, f32[104,128]{1,0:T(8,128)S(1)}, u32[]{:S(2)}, u32[]{:S(2)}) collective-permute-start(f32[104,128]{1,0:T(8,128)S(1)} %get-tuple-element.20), channel_id=1, source_target_pairs={{0,32},{32,64},{64,96},{96,128},{128,160},{160,192},{192,224},{224... | collective-permute-start | bytes 159752 | tf_op jit(solution)/shard_map/ppermute | solution.py:533
  14.0 10.7 %collective-permute-start.1 = (f32[104,128]{1,0:T(8,128)S(1)}, f32[104,128]{1,0:T(8,128)S(1)}, u32[]{:S(2)}, u32[]{:S(2)}) collective-permute-start(f32[104,128]{1,0:T(8,128)S(1)} %get-tuple-element.21), channel_id=1, source_target_pairs={{0,992},{32,0},{64,32},{96,64},{128,96},{160,128},{192,160},{224,1... | collective-permute-start | bytes 159752 | tf_op jit(solution)/shard_map/ppermute | solution.py:533
  24.7 19.3 %copy-start.1 = (f32[256,64]{0,1:T(8,128)S(1)}, f32[256,64]{0,1:T(8,128)}, u32[]{:S(2)}) copy-start(f32[256,64]{0,1:T(8,128)} %param.22) | copy-start | bytes 196612
  24.7 19.3 %copy-start.2 = (f32[64,64]{1,0:T(8,128)S(1)}, f32[64,64]{1,0:T(8,128)}, u32[]{:S(2)}) copy-start(f32[64,64]{1,0:T(8,128)} %wl.1) | copy-start | bytes 49156
  24.7 19.4 %copy-start.3 = (f32[64,64]{1,0:T(8,128)S(1)}, f32[64,64]{1,0:T(8,128)}, u32[]{:S(2)}) copy-start(f32[64,64]{1,0:T(8,128)} %we.1) | copy-start | bytes 49156
  24.7 19.4 %copy-start.5 = (f32[12,64]{1,0:T(8,128)S(1)}, f32[12,64]{1,0:T(8,128)}, u32[]{:S(2)}) copy-start(f32[12,64]{1,0:T(8,128)} %w2.1) | copy-start | bytes 9220
  24.8 20.1 %collective-permute-start.2 = (f32[208,128]{1,0:T(8,128)S(1)}, f32[208,128]{1,0:T(8,128)S(1)}, u32[]{:S(2)}, u32[]{:S(2)}) collective-permute-start(f32[208,128]{1,0:T(8,128)S(1)} %get-tuple-element.23), channel_id=1, source_target_pairs={{0,4},{4,8},{8,12},{12,16},{16,20},{20,24},{24,28},{28,0},{1,5},{5... | collective-permute-start | bytes 319496 | tf_op jit(solution)/shard_map/ppermute | solution.py:533
  29.9 16.3 %collective-permute-start.3 = (f32[208,128]{1,0:T(8,128)S(1)}, f32[208,128]{1,0:T(8,128)S(1)}, u32[]{:S(2)}, u32[]{:S(2)}) collective-permute-start(f32[208,128]{1,0:T(8,128)S(1)} %get-tuple-element.24), channel_id=1, source_target_pairs={{0,28},{4,0},{8,4},{12,8},{16,12},{20,16},{24,20},{28,24},{1,29},{... | collective-permute-start | bytes 319496 | tf_op jit(solution)/shard_map/ppermute | solution.py:533
  44.0 0.7 %copy-start.6 = (f32[64]{0:T(128)S(1)}, f32[64]{0:T(128)}, u32[]{:S(2)}) copy-start(f32[64]{0:T(128)} %param.23) | copy-start | bytes 772
  44.7 1.6 %copy-start.4 = (bf16[128,128]{1,0:T(8,128)(2,1)S(1)}, bf16[128,128]{1,0:T(8,128)(2,1)}, u32[]{:S(2)}) copy-start(bf16[128,128]{1,0:T(8,128)(2,1)} %constant.9.clone.fp_ref) | copy-start | bytes 98308

commit v2 on v1

--- a/solution.py
+++ b/solution.py
@@ -16,9 +16,9 @@
 SM = pl.BlockSpec(memory_space=pltpu.SMEM)
 HB = pl.BlockSpec(memory_space=pltpu.HBM)
 NS = 16
-NB = 64
-PAIRS = 32 * NB
-TILES = PAIRS // 128
+TILES = 12
+PAIRS = 128 * TILES
+FULL = 42
 LIST = 40
 
 
@@ -184,11 +184,14 @@
     return jnp.concatenate([h, l, h], axis=0)
 
 
+def tree(parts):
+    while len(parts) > 1:
+        parts = [a + b for a, b in zip(parts[0::2], parts[1::2])] + parts[len(parts) & ~1 :]
+    return parts[0]
+
+
 def fold(v):
-    parts = [v[:, 128 * i : 128 * i + 128] for i in range(TILES)]
-    while len(parts) > 1:
-        parts = [a + b for a, b in zip(parts[0::2], parts[1::2])]
-    return parts[0]
+    return tree([v[:, 128 * i : 128 * i + 128] for i in range(TILES)])
 
 
 def wide(v):
@@ -247,7 +250,7 @@
     o_ref, la_ref, xm_ref, xp_ref, ym_ref, yp_ref,
     t2, tl, te, to, bo, be, bl, b2, rc, fp_ref,
     en_ref, fo_ref,
-    w_s, q_s, g_s, a_s, in_s, dw_s, sc_s, tb_s, ls_s, rk_s, acc_s, out_s, b_s,
+    w_s, g_s, a_s, in_s, dw_s, sc_s, tb_s, ls_s, rk_s, acc_s, out_s, b_s, y_s, d_s,
 ):
     halves = []
     for h in range(2):
@@ -259,20 +262,12 @@
             axis=0,
         )
         halves.append(v.T[0:96])
-    tb_s[...] = jnp.concatenate(split(jnp.concatenate(halves, axis=0), 2), axis=0)
+    tb_s[...] = jnp.concatenate(split(jnp.concatenate(halves, axis=0), 2), axis=1)
 
     places = [(la_ref, 0), (la_ref, LIST), (ym_ref, 128), (ym_ref, 128 + LIST), (yp_ref, 128), (yp_ref, 128 + LIST)]
-    (dx, dy, dz), _, _, _ = tiles((1, 768))
     lst = jnp.concatenate([ref[at : at + LIST, :] for ref, at in places], axis=1)
     high = jnp.floor(lst[0:33] * (1.0 / 64.0))
     low = lst[0:33] - 64.0 * high
-    ls_s[...] = jnp.concatenate(
-        [
-            high[0:32], low[0:32], high[32:33], low[32:33], lst[33:34],
-            dx + 1.0, dy + 1.0, dz + 1.0, jnp.zeros((10, 768), F32),
-        ],
-        axis=0,
-    ).astype(BF16)
     (dx, dy, dz), valid, own, lane = tiles((8, 128))
     pad = jnp.zeros((2, 128), F32)
     ce = jnp.concatenate([ref[at + 32 : at + 33, :] for ref, at in places] + [pad], axis=0)
@@ -282,51 +277,81 @@
     for c, d in ((cx, dx), (cy, dy), (cz, dz)):
         v = c + 8.0 * d
         flag = flag & (v >= -2.0) & (v < 10.0)
+    mine = jnp.where(own & (ct > 0.0), 1.0, 0.0)
     flag = jnp.where(flag, 1.0, 0.0)
+    units = div(ct + (TILES - 1.0), TILES)
     tri = lax.broadcasted_iota(jnp.int32, (128, 128), 0) <= lax.broadcasted_iota(
         jnp.int32, (128, 128), 1
     )
-    upto = mm(flag.astype(BF16), jnp.where(tri, 1.0, 0.0).astype(BF16))
-    total = jnp.broadcast_to(jnp.sum(flag, axis=1, keepdims=True), (8, 128))
+    both = jnp.concatenate([units * flag, flag, units * mine, mine], axis=0)
+    upto = mm(both.astype(BF16), jnp.where(tri, 1.0, 0.0).astype(BF16))
+    total = jnp.broadcast_to(jnp.sum(both, axis=1, keepdims=True), (32, 128))
     row = lax.broadcasted_iota(jnp.int32, (8, 128), 0)
-    before = jnp.where(row >= 1, pltpu.roll(total, 1, axis=0), 0.0)
-    for by in (1, 2, 4):
-        before = before + jnp.where(row >= by, pltpu.roll(before, by, axis=0), 0.0)
-    mine = own & (ct > 0.0)
-    owned = jnp.sum(jnp.where(mine, 1.0, 0.0))
-    rank = jnp.where(flag > 0.0, upto + before + (owned - 1.0), -1.0)
-    rk_s[...] = jnp.where(mine, (lane - 16).astype(F32), rank)
-    blocks = lax.div((owned + jnp.sum(flag)).astype(jnp.int32) + (NB - 1), NB)
+
+    def running(k):
+        t = jnp.where(row >= 1, pltpu.roll(total[8 * k : 8 * k + 8], 1, axis=0), 0.0)
+        for by in (1, 2, 4):
+            t = t + jnp.where(row >= by, pltpu.roll(t, by, axis=0), 0.0)
+        return upto[8 * k : 8 * k + 8] + t
+
+    def start(k):
+        o = upto[8 * k + 16 : 8 * k + 24] - both[8 * k + 16 : 8 * k + 24]
+        g = running(k) - both[8 * k : 8 * k + 8] + total[8 * k + 16 : 8 * k + 17]
+        return jnp.where(mine > 0.0, o, g)
+
+    needed = jnp.sum(both[0:8]) + jnp.sum(both[16:24])
+    listed = jnp.sum(both[8:16]) + jnp.sum(both[24:32])
+    fits = needed <= 128.0
+    index = start(1)
+    block_of = div(index, FULL)
+    rank = jnp.where(fits, start(0), 128.0 * block_of + 3.0 * (index - FULL * block_of))
+    used = (mine + flag) > 0.0
+    rk_s[0:8, :] = jnp.where(used, rank, 1e6)
+    rk_s[8:16, :] = jnp.where(used, rank + jnp.where(fits, units, 3.0), 0.0)
+    blocks = jnp.where(fits, 1, lax.div(listed.astype(jnp.int32) + (FULL - 1), FULL))
+    rank = jnp.where(used, rank, 0.0)
+    at = jnp.concatenate([rank[t : t + 1] for t in range(6)], axis=1)
+    (dx, dy, dz), _, _, _ = tiles((1, 768))
+    ls_s[...] = jnp.concatenate(
+        [
+            high[0:32], low[0:32], high[32:33], low[32:33], lst[33:34],
+            dx + 1.0, dy + 1.0, dz + 1.0, jnp.floor(at * (1.0 / 64.0)), at - 64.0 * jnp.floor(at * (1.0 / 64.0)),
+            jnp.zeros((8, 768), F32),
+        ],
+        axis=0,
+    ).astype(BF16)
     acc_s[...] = jnp.zeros((64, 128), F32)
     sc_s[...] = jnp.zeros((8, PAIRS + 128), F32)
     in_s[12:16, :] = jnp.zeros((4, PAIRS), F32)
 
-    apart = lax.broadcasted_iota(jnp.int32, (128, 128), 0) - lax.broadcasted_iota(
-        jnp.int32, (128, 128), 1
-    )
-    comb = jnp.where((apart & (NB - 1)) == 0, 1.0, 0.0).astype(BF16)
-
-    def slots_sum(v):
-        r = mm(jnp.concatenate(split(v, 2), axis=0), comb)
-        return r[0:576] + r[576:1152]
-
     def block(b, carry):
-        want = (lax.broadcasted_iota(jnp.int32, (128, 128), 0) & (NB - 1)) + NB * b
-        want = want.astype(F32)
+        want = (lax.broadcasted_iota(jnp.int32, (128, 128), 0) + 128 * b).astype(F32)
         chosen = jnp.concatenate(
-            [jnp.where(want == rk_s[t : t + 1, :], 1.0, 0.0).astype(BF16) for t in range(6)], axis=1
+            [
+                jnp.where(
+                    (want >= rk_s[t : t + 1, :]) & (want < rk_s[8 + t : 9 + t, :]), 1.0, 0.0
+                ).astype(BF16)
+                for t in range(6)
+            ],
+            axis=1,
         )
         u = mm(ls_s[...], chosen, ((1,), (1,)))
-        left = lax.broadcasted_iota(jnp.int32, (1, 128), 1) < NB
+        key = 64.0 * u[70:71] + u[71:72]
+        part = (lax.broadcasted_iota(jnp.int32, (1, 128), 1) + 128 * b).astype(F32) - key
+        keys = jnp.broadcast_to(key, (128, 128))
+        comb = jnp.where(keys == keys.T, 1.0, 0.0).astype(BF16)
+        comb = jnp.concatenate([comb, comb], axis=0)
+
+        def slots_sum(v):
+            return mm(jnp.concatenate(split(v, 2), axis=1), comb)
 
         def slots(at):
-            return jnp.concatenate(
-                [
-                    jnp.where(left, u[at + 2 * g : at + 2 * g + 1], u[at + 2 * g + 1 : at + 2 * g + 2])
-                    for g in range(TILES)
-                ],
-                axis=1,
-            )
+            def pick_slot(t):
+                v = [u[at + t + k : at + t + k + 1] for k in (0, TILES, 2 * TILES) if t + k < 32]
+                late = v[2] if len(v) > 2 else jnp.zeros((1, 128), F32)
+                return jnp.where(part < 0.5, v[0], jnp.where(part < 1.5, v[1], late))
+
+            return jnp.concatenate([pick_slot(t) for t in range(TILES)], axis=1)
 
         nb = 64.0 * slots(0) + slots(32)
         ce = 64.0 * u[64:65] + u[65:66]
@@ -344,24 +369,23 @@
         q = q + wide(shift[1] - 2.0)
         s = s + wide(shift[2] - 2.0)
         lane = lax.broadcasted_iota(jnp.int32, (1, PAIRS), 1)
-        alive = lax.div(lane, NB).astype(F32) < wide(count)
+        alive = lax.shift_right_logical(lane, 7).astype(F32) < wide(count - TILES * part)
         live = jnp.where(alive, 1.0, 0.0)
         second = place(p, q, s, a)
         centre = place(cx, cy, cz, ca)
         geo = [second[k] - wide(centre[k]) for k in range(3)]
         rows = jnp.concatenate([table_row(p + 4.0, q + 4.0), table_row(cx + 4.0, cy + 4.0)], axis=1)
         rsel = jnp.concatenate([3.0 * (s + 4.0) + a, 3.0 * (cz + 4.0) + ca], axis=1)
-        at = lax.broadcasted_iota(jnp.int32, (256, PAIRS + 128), 0).astype(F32)
-        hot = jnp.where(at == rows, 1.0, 0.0).astype(BF16)
-
-        got = mm(tb_s[...], hot)
+        at = lax.broadcasted_iota(jnp.int32, (256, PAIRS + 128), 0).astype(F32).astype(BF16)
+        hot = jnp.where(at == jnp.broadcast_to(rows.astype(BF16), at.shape), jnp.ones_like(at), jnp.zeros_like(at))
+
+        got = mm(tb_s[...], jnp.concatenate([hot, hot], axis=0))
         half = lax.shift_right_logical(
             lax.broadcasted_iota(jnp.int32, (8, PAIRS + 128), 0), 2
         ).astype(F32)
         pick = jnp.zeros((8, PAIRS + 128), F32)
         for k in range(24):
-            v = got[8 * k : 8 * k + 8] + got[192 + 8 * k : 200 + 8 * k]
-            pick = jnp.where(half + 2.0 * k == rsel, v, pick)
+            pick = jnp.where(half + 2.0 * k == rsel, got[8 * k : 8 * k + 8], pick)
         pick = pick[0:4] + pick[4:8]
         first = wide(pick[:, PAIRS:])
         second = pick[:, 0:PAIRS]
@@ -418,75 +442,95 @@
             None, R3 * ux, R3 * uy, R3 * uz, R15 * ux * uy, R15 * uy * uz,
             (0.5 * R5) * (3.0 * uz * uz - 1.0), R15 * ux * uz, (0.5 * R15) * (ux * ux - uy * uy),
         ]
-        yb = [None] + [jnp.broadcast_to(v, (8, PAIRS)) for v in ys[1:]]
-        for c in range(8):
-            at = slice(8 * c, 8 * c + 8)
-            w = w_s[at, :]
-            for m in range(9):
-                a_s[m, at, :] = 0.2 * fold(w if m == 0 else w * yb[m])
-        a_s[...] = slots_sum(a_s[...].reshape(576, 128)).reshape(9, 64, 128)
-        for c in range(8):
-            at = slice(8 * c, 8 * c + 8)
-            sums = [None, None, None]
-            for m in range(9):
-                am = wide(a_s[m, at, :])
-                term = am if m == 0 else yb[m] * am
-                l = ORDER[m]
-                sums[l] = term if sums[l] is None else sums[l] + term
-            for l in range(3):
-                q_s[l, at, :] = sums[l]
-        wv = w_s[...]
-        joined = jnp.concatenate([z] + [wv * q_s[l] for l in range(3)], axis=0)
+        for m in range(1, 9):
+            y_s[m : m + 1, :] = ys[m]
+
+        def each_group(make):
+            def run(c, carry):
+                at = slice(8 * c, 8 * c + 8)
+                for l, first_m, last_m in ((0, 0, 1), (1, 1, 4), (2, 4, 9)):
+                    v = [make(at, c, l, i) for i in range(TILES)]
+                    for m in range(first_m, last_m):
+                        b_s[m, at, :] = 0.2 * tree(
+                            [
+                                v[i] if m == 0 else v[i] * y_s[m : m + 1, 128 * i : 128 * i + 128]
+                                for i in range(TILES)
+                            ]
+                        )
+                return carry
+
+            for c in range(8):
+                run(c, 0)
+            return slots_sum(b_s[...].reshape(576, 128)).reshape(9, 64, 128)
+
+        a_s[...] = each_group(lambda at, c, l, i: w_s[at, 128 * i : 128 * i + 128])
+
+        def weigh(i, carry):
+            at = slice(128 * i, 128 * i + 128)
+            yt = [None] + [jnp.broadcast_to(y_s[m : m + 1, at], (8, 128)) for m in range(1, 9)]
+            for c in range(8):
+                rows = slice(8 * c, 8 * c + 8)
+                sums = [None, None, None]
+                for m in range(9):
+                    term = a_s[m, rows, :] if m == 0 else yt[m] * a_s[m, rows, :]
+                    l = ORDER[m]
+                    sums[l] = term if sums[l] is None else sums[l] + term
+                for l in range(3):
+                    g_s[64 * l + 8 * c : 64 * l + 8 * c + 8, at] = sums[l] * w_s[rows, at]
+            return carry
+
+        for i in range(TILES):
+            weigh(i, 0)
+        joined = jnp.concatenate([z, g_s[...]], axis=0)
         y, dy_ = silu(mm(to[...], stack3(joined)))
         ro = rc[...]
         raw = jnp.sum(ro * y, axis=0, keepdims=True)
 
         @pl.when(b == 0)
         def _():
-            en = fold(raw * ev)
-            en = en + pltpu.roll(en, NB, axis=1)
-            first_lanes = lax.broadcasted_iota(jnp.int32, (1, 128), 1).astype(F32)
-            en = jnp.where(first_lanes < owned, en, 0.0)
-            en_ref[...] = en[:, 0:NS].reshape(1, 1, NS)
+            en = jnp.concatenate(split(fold(raw * ev), 3) + [jnp.zeros((5, 128), BF16)], axis=0)
+            en = jnp.sum(mm(en, chosen[:, 0:128]), axis=0, keepdims=True)
+            en_ref[...] = en[:, NS : 2 * NS].reshape(1, 1, NS)
 
         denv = live * raw
         dj = mm(bo[...], stack3((ro * ev) * dy_))
         g_s[...] = dj[64:256]
-        for c in range(8):
-            at = slice(8 * c, 8 * c + 8)
-            w = w_s[at, :]
-            for l in range(3):
-                gw = g_s[64 * l + 8 * c : 64 * l + 8 * c + 8, :] * w
+
+        def grown(at, c, l, i):
+            tile = slice(128 * i, 128 * i + 128)
+            return g_s[64 * l + 8 * c : 64 * l + 8 * c + 8, tile] * w_s[at, tile]
+
+        b_s[...] = each_group(grown)
+
+        def back(i, carry):
+            at = slice(128 * i, 128 * i + 128)
+            yt = [None] + [jnp.broadcast_to(y_s[m : m + 1, at], (8, 128)) for m in range(1, 9)]
+            acc = [None] * 9
+            for c in range(8):
+                rows = slice(8 * c, 8 * c + 8)
+                w = w_s[rows, at]
+                g = [g_s[64 * l + 8 * c : 64 * l + 8 * c + 8, at] for l in range(3)]
+                dw = None
                 for m in range(9):
-                    if ORDER[m] == l:
-                        b_s[m, at, :] = 0.2 * fold(gw if m == 0 else gw * yb[m])
-        b_s[...] = slots_sum(b_s[...].reshape(576, 128)).reshape(9, 64, 128)
-        acc = [None] * 9
-        for c in range(8):
-            at = slice(8 * c, 8 * c + 8)
-            w = w_s[at, :]
-            dw = None
-            for l in range(3):
-                g = g_s[64 * l + 8 * c : 64 * l + 8 * c + 8, :]
-                part = g * q_s[l, at, :]
-                dw = part if dw is None else dw + part
-                gw = g * w
-                for m in range(9):
-                    if ORDER[m] != l:
-                        continue
-                    bm = wide(b_s[m, at, :])
-                    dw = dw + (bm if m == 0 else yb[m] * bm)
+                    t = g[ORDER[m]] * a_s[m, rows, :] + b_s[m, rows, :]
+                    v = t if m == 0 else yt[m] * t
+                    dw = v if dw is None else dw + v
                     if m:
-                        v = gw * wide(a_s[m, at, :]) + w * bm
-                        acc[m] = v if acc[m] is None else acc[m] + v
-            dw_s[at, :] = dw
+                        acc[m] = w * t if acc[m] is None else acc[m] + w * t
+                dw_s[rows, at] = dw
+            for m in range(1, 9):
+                d_s[m : m + 1, at] = jnp.sum(acc[m], axis=0, keepdims=True)
+            return carry
+
+        for i in range(TILES):
+            back(i, 0)
         dw = dw_s[...]
         denv = denv + live * jnp.sum(dw * e, axis=0, keepdims=True)
         dz = dj[0:64] + mm(be[...], stack3(dw * ev))
         dh = mm(bl[...], stack3(dz * dz_))
         db = mm(b2[...], stack3(dh * dh_))
         dd = denv * denv_dd + jnp.sum(db * dbasis, axis=0, keepdims=True)
-        dy = [None] + [jnp.sum(acc[m], axis=0, keepdims=True) for m in range(1, 9)]
+        dy = [None] + [d_s[m : m + 1, :] for m in range(1, 9)]
         du0 = R3 * dy[1] + R15 * (uy * dy[4] + uz * dy[7] + ux * dy[8])
         du1 = R3 * dy[2] + R15 * (ux * dy[4] + uz * dy[5] - uy * dy[8])
         du2 = R3 * dy[3] + R15 * (uy * dy[5] + ux * dy[7]) + (3.0 * R5) * uz * dy[6]
@@ -506,7 +550,8 @@
         )
         mh, ml = split(m, 2)
         nt = ((1,), (1,))
-        acc_s[...] += mm(hot[0:64], mh, nt) + mm(hot[0:64], ml, nt)
+        own = hot[0:64]
+        acc_s[...] += mm(jnp.concatenate([own, own], axis=1), jnp.concatenate([mh, ml], axis=1), nt)
         return carry
 
     lax.fori_loop(0, blocks, block, 0)
@@ -588,13 +633,13 @@
         [(v, VM) for v in (own, lists, xm, xp, ym, yp, *ws, jnp.asarray(fperm(), BF16))],
         "pairs",
         [
-            pltpu.VMEM((64, PAIRS), F32), pltpu.VMEM((3, 64, PAIRS), F32),
+            pltpu.VMEM((64, PAIRS), F32),
             pltpu.VMEM((192, PAIRS), F32), pltpu.VMEM((9, 64, 128), F32),
             pltpu.VMEM((16, PAIRS), F32), pltpu.VMEM((64, PAIRS), F32),
-            pltpu.VMEM((8, PAIRS + 128), F32), pltpu.VMEM((384, 256), BF16),
-            pltpu.VMEM((80, 768), BF16), pltpu.VMEM((8, 128), F32),
+            pltpu.VMEM((8, PAIRS + 128), F32), pltpu.VMEM((192, 512), BF16),
+            pltpu.VMEM((80, 768), BF16), pltpu.VMEM((16, 128), F32),
             pltpu.VMEM((64, 128), F32), pltpu.VMEM((64, 128), F32),
-            pltpu.VMEM((9, 64, 128), F32),
+            pltpu.VMEM((9, 64, 128), F32), pltpu.VMEM((16, PAIRS), F32), pltpu.VMEM((16, PAIRS), F32),
         ],
         mib=24,
     )

time: 54.1 us -> 53.1 us (0.982)
  Pallas kernels: 9.15 us -> 8.1 us
    pallas_call x5, Pallas kernels: 9.15 us -> 8.1 us  [call(): pl.pallas_call(kernel, out_shape=outs, in_specs=specs, out_specs=jax.tree...]
where the time goes in v2:
time: 53.1 us; the launch traced here: 52.8 us
  starting transfers between devices  26.9 us (51%)
  waiting for transfers between devices  10.1 us (19%)
  Pallas kernels  8.1 us (15%)
  blocking collectives  5.55 us (10%)
  between operations  1.45 us (3%)
  local copies, waits for them, and re-layouts  0.64 us (1%)
    ppermute x4, starting transfers between devices, hop(): return lax.ppermute(v, axis, [(i, (i + by) % n) for i in range(n)])  26.9 us
    ppermute x4, waiting for transfers between devices, hop(): return lax.ppermute(v, axis, [(i, (i + by) % n) for i in range(n)])  10.1 us
    pallas_call x5, Pallas kernels, call(): pl.pallas_call(kernel, out_shape=outs, in_specs=specs, out_specs=jax.tree...  8.1 us
    all_gather x1, blocking collectives, local(): column = lax.all_gather(flat, 'gz')  5.55 us
  transfers between devices with their start and end apart: 4, of which 2 were waited for; matrix products, arithmetic and copies ran while one was open for 0% of the time, Pallas kernels for 0%

profile of v2, /device:TPU:46, one launch (start us, length us, event | category | flops | bytes accessed | tf_op | source)
XLA Modules:
  0.0 52.8 jit_solution(3836039020488721454)
XLA Ops:
  0.6 0.0 copy-start
  1.3 0.9 %pack.1 = f32[88,128]{1,0:T(8,128)S(1)} custom-call(f32[1,1,4608]{2,1,0:T(1,128)} %d_in.1, s32[1,1,1536]{2,1,0:T(1,128)} %s_in.1, s32[1,1,512]{2,1,0:T(1,128)} %nb_in.1, s32[1,1,16]{2,1,0:T(1,128)} %ce_in.1, s32[1,1,16]{2,1,0:T(1,128)} %ct_in.1, s32[1]{0:T(128)} %bitcast.5.al_ref), custom_call_target="tpu_custom_call" | custom-call | tf_op jit(solution)/shard_map/pack/pallas_call | solution.py:27
  2.3 5.6 %all-gather = f32[352,128]{1,0:T(8,128)S(1)} all-gather(f32[88,128]{1,0:T(8,128)S(1)} %pack.1), channel_id=2, replica_groups=mesh['gx'=32,'gy'=8,'gz'=4] {'gz'}, dimensions={0}, use_global_device_ids=true | all-gather | bytes 225280 | tf_op jit(solution)/shard_map/all_gather | solution.py:602
  7.8 0.0 copy-done
  7.8 0.4 zrows.1
  8.2 5.7 %collective-permute-start = (f32[104,128]{1,0:T(8,128)S(1)}, f32[104,128]{1,0:T(8,128)S(1)}, u32[]{:S(2)}, u32[]{:S(2)}) collective-permute-start(f32[104,128]{1,0:T(8,128)S(1)} %get-tuple-element.20), channel_id=1, source_target_pairs={{0,32},{32,64},{64,96},{96,128},{128,160},{160,192},{192,224},{224... | collective-permute-start | bytes 159752 | tf_op jit(solution)/shard_map/ppermute | solution.py:578
  14.0 1.9 %collective-permute-start.1 = (f32[104,128]{1,0:T(8,128)S(1)}, f32[104,128]{1,0:T(8,128)S(1)}, u32[]{:S(2)}, u32[]{:S(2)}) collective-permute-start(f32[104,128]{1,0:T(8,128)S(1)} %get-tuple-element.21), channel_id=1, source_target_pairs={{0,992},{32,0},{64,32},{96,64},{128,96},{160,128},{192,160},{224,1... | collective-permute-start | bytes 159752 | tf_op jit(solution)/shard_map/ppermute | solution.py:578
  15.9 0.0 collective-permute-done.m_ref.xm_ref
  15.9 8.8 %collective-permute-done.1.p_ref.xp_ref = f32[104,128]{1,0:T(8,128)S(1)} collective-permute-done((f32[104,128]{1,0:T(8,128)S(1)}, f32[104,128]{1,0:T(8,128)S(1)}, u32[]{:S(2)}, u32[]{:S(2)}) %collective-permute-start.1) | collective-permute-done | bytes 53280 | tf_op jit(solution)/shard_map/ppermute | solution.py:578
  24.7 0.0 copy-start.1
  24.7 0.0 copy-start.2
  24.7 0.0 copy-start.3
  24.7 0.0 copy-start.5
  24.7 0.1 yslab.1
  24.8 5.2 %collective-permute-start.2 = (f32[208,128]{1,0:T(8,128)S(1)}, f32[208,128]{1,0:T(8,128)S(1)}, u32[]{:S(2)}, u32[]{:S(2)}) collective-permute-start(f32[208,128]{1,0:T(8,128)S(1)} %get-tuple-element.23), channel_id=1, source_target_pairs={{0,4},{4,8},{8,12},{12,16},{16,20},{20,24},{24,28},{28,0},{1,5},{5... | collective-permute-start | bytes 319496 | tf_op jit(solution)/shard_map/ppermute | solution.py:578
  29.9 14.0 %collective-permute-start.3 = (f32[208,128]{1,0:T(8,128)S(1)}, f32[208,128]{1,0:T(8,128)S(1)}, u32[]{:S(2)}, u32[]{:S(2)}) collective-permute-start(f32[208,128]{1,0:T(8,128)S(1)} %get-tuple-element.24), channel_id=1, source_target_pairs={{0,28},{4,0},{8,4},{12,8},{16,12},{20,16},{24,20},{28,24},{1,29},{... | collective-permute-start | bytes 319496 | tf_op jit(solution)/shard_map/ppermute | solution.py:578
  44.0 0.0 copy-start.6
  44.0 0.0 copy-done.1
  44.0 0.0 copy-done.2
  44.0 0.0 copy-done.3
  44.0 0.0 copy-done.5
  44.1 0.6 %copy-done.6 = f32[64]{0:T(128)S(1)} copy-done((f32[64]{0:T(128)S(1)}, f32[64]{0:T(128)}, u32[]{:S(2)}) %copy-start.6) | copy-done | bytes 280
  44.7 0.0 copy-start.4
  44.7 0.2 weights.1
  44.9 0.0 collective-permute-done.2.ym_ref
  44.9 1.4 %collective-permute-done.3.yp_ref = f32[208,128]{1,0:T(8,128)S(1)} collective-permute-done((f32[208,128]{1,0:T(8,128)S(1)}, f32[208,128]{1,0:T(8,128)S(1)}, u32[]{:S(2)}, u32[]{:S(2)}) %collective-permute-start.3) | collective-permute-done | bytes 106528 | tf_op jit(solution)/shard_map/ppermute | solution.py:578
  46.3 0.0 copy-done.4
  46.3 6.5 %pairs.1 = (f32[1,1,16]{2,1,0:T(1,128)}, f32[1,1,4608]{2,1,0:T(1,128)}) custom-call(f32[2,64,128]{2,1,0:T(8,128)S(1)} %get-tuple-element.18.o_ref, f32[80,128]{1,0:T(8,128)S(1)} %get-tuple-element.22.la_ref, f32[104,128]{1,0:T(8,128)S(1)} %collective-permute-done.m_ref.xm_ref, f32[104,128]{1,0:T(8,128)S(1)} %collective-permute-done.1.p_ref.xp_ref, ...), custom_call_target="tpu_custom_call" | custom-call | tf_op jit(solution)/shard_map/pairs/pallas_call | solution.py:27
Async XLA Ops:
  0.6 7.2 %copy-start = (bf16[384,256]{1,0:T(8,128)(2,1)S(1)}, bf16[384,256]{1,0:T(8,128)(2,1)}, u32[]{:S(2)}) copy-start(bf16[384,256]{1,0:T(8,128)(2,1)} %constant.8.clone.p_ref) | copy-start | bytes 589828
  8.2 7.7 %collective-permute-start = (f32[104,128]{1,0:T(8,128)S(1)}, f32[104,128]{1,0:T(8,128)S(1)}, u32[]{:S(2)}, u32[]{:S(2)}) collective-permute-start(f32[104,128]{1,0:T(8,128)S(1)} %get-tuple-element.20), channel_id=1, source_target_pairs={{0,32},{32,64},{64,96},{96,128},{128,160},{160,192},{192,224},{224... | collective-permute-start | bytes 159752 | tf_op jit(solution)/shard_map/ppermute | solution.py:578
  14.0 10.7 %collective-permute-start.1 = (f32[104,128]{1,0:T(8,128)S(1)}, f32[104,128]{1,0:T(8,128)S(1)}, u32[]{:S(2)}, u32[]{:S(2)}) collective-permute-start(f32[104,128]{1,0:T(8,128)S(1)} %get-tuple-element.21), channel_id=1, source_target_pairs={{0,992},{32,0},{64,32},{96,64},{128,96},{160,128},{192,160},{224,1... | collective-permute-start | bytes 159752 | tf_op jit(solution)/shard_map/ppermute | solution.py:578
  24.7 19.3 %copy-start.1 = (f32[256,64]{0,1:T(8,128)S(1)}, f32[256,64]{0,1:T(8,128)}, u32[]{:S(2)}) copy-start(f32[256,64]{0,1:T(8,128)} %param.22) | copy-start | bytes 196612
  24.7 19.3 %copy-start.2 = (f32[64,64]{1,0:T(8,128)S(1)}, f32[64,64]{1,0:T(8,128)}, u32[]{:S(2)}) copy-start(f32[64,64]{1,0:T(8,128)} %wl.1) | copy-start | bytes 49156
  24.7 19.4 %copy-start.3 = (f32[64,64]{1,0:T(8,128)S(1)}, f32[64,64]{1,0:T(8,128)}, u32[]{:S(2)}) copy-start(f32[64,64]{1,0:T(8,128)} %we.1) | copy-start | bytes 49156
  24.7 19.4 %copy-start.5 = (f32[12,64]{1,0:T(8,128)S(1)}, f32[12,64]{1,0:T(8,128)}, u32[]{:S(2)}) copy-start(f32[12,64]{1,0:T(8,128)} %w2.1) | copy-start | bytes 9220
  24.8 20.1 %collective-permute-start.2 = (f32[208,128]{1,0:T(8,128)S(1)}, f32[208,128]{1,0:T(8,128)S(1)}, u32[]{:S(2)}, u32[]{:S(2)}) collective-permute-start(f32[208,128]{1,0:T(8,128)S(1)} %get-tuple-element.23), channel_id=1, source_target_pairs={{0,4},{4,8},{8,12},{12,16},{16,20},{20,24},{24,28},{28,0},{1,5},{5... | collective-permute-start | bytes 319496 | tf_op jit(solution)/shard_map/ppermute | solution.py:578
  29.9 16.3 %collective-permute-start.3 = (f32[208,128]{1,0:T(8,128)S(1)}, f32[208,128]{1,0:T(8,128)S(1)}, u32[]{:S(2)}, u32[]{:S(2)}) collective-permute-start(f32[208,128]{1,0:T(8,128)S(1)} %get-tuple-element.24), channel_id=1, source_target_pairs={{0,28},{4,0},{8,4},{12,8},{16,12},{20,16},{24,20},{28,24},{1,29},{... | collective-permute-start | bytes 319496 | tf_op jit(solution)/shard_map/ppermute | solution.py:578
  44.0 0.7 %copy-start.6 = (f32[64]{0:T(128)S(1)}, f32[64]{0:T(128)}, u32[]{:S(2)}) copy-start(f32[64]{0:T(128)} %param.23) | copy-start | bytes 772
  44.7 1.6 %copy-start.4 = (bf16[128,128]{1,0:T(8,128)(2,1)S(1)}, bf16[128,128]{1,0:T(8,128)(2,1)}, u32[]{:S(2)}) copy-start(bf16[128,128]{1,0:T(8,128)(2,1)} %constant.9.clone.fp_ref) | copy-start | bytes 98308
